TPU v7x, 32 devices: a whole 2x2x4 slice. The times are simulated.
32 devices in a mesh: seq: 4 (over y, x), wshard: 8 (over z, core).
Axes of the slice: x: 2, y: 2, z: 4, core: 2. Of those that a mesh axis runs over, the one named last changes fastest.
Arguments:
- layer_input: bfloat16 [8, 1024, 1536], P('wshard', 'seq'), may hold values from -6 to 6
- lengths: int32 [8], P('wshard'), may hold values from 256 to 1024, as said below
- norm_attn: float32 [1536], replicated, may hold values from 0.1 to 1.9
- w_query: bfloat16 [1536, 1536], P('wshard'), may hold values from -0.15625 to 0.15625
- w_key: bfloat16 [1536, 1536], P('wshard'), may hold values from -0.15625 to 0.15625
- w_value: bfloat16 [1536, 1536], P('wshard'), may hold values from -0.15625 to 0.15625
- w_ogate: bfloat16 [1536, 1536], P('wshard'), may hold values from -0.15625 to 0.15625
- w_forget: bfloat16 [1536, 24], P('wshard'), may hold values from -0.15625 to 0.15625
- forget_bias: float32 [24], replicated, may hold values from 3.5 to 8
- w_out: bfloat16 [1536, 1536], P('wshard'), may hold values from -1 to 1
- norm_ffn: float32 [1536], replicated, may hold values from 0.1 to 1.9
- w_gate: bfloat16 [1536, 4096], P('wshard'), may hold values from -0.15625 to 0.15625
- w_up: bfloat16 [1536, 4096], P('wshard'), may hold values from -0.15625 to 0.15625
- w_down: bfloat16 [4096, 1536], P('wshard'), may hold values from -0.09375 to 0.09375
- output_grad: bfloat16 [8, 1024, 1536], P('wshard', 'seq'), may hold values from -6 to 6
Outputs:
- layer_output: bfloat16 [8, 1024, 1536], P('wshard', 'seq')
- grad_input: float32 [8, 1024, 1536], P('wshard', 'seq')
- grad_norm_attn: float32 [1536], replicated
- grad_w_query: float32 [1536, 1536], P('wshard')
- grad_w_key: float32 [1536, 1536], P('wshard')
- grad_w_value: float32 [1536, 1536], P('wshard')
- grad_w_ogate: float32 [1536, 1536], P('wshard')
- grad_w_forget: float32 [1536, 24], P('wshard')
- grad_forget_bias: float32 [24], replicated
- grad_w_out: float32 [1536, 1536], P('wshard')
- grad_norm_ffn: float32 [1536], replicated
- grad_w_gate: float32 [1536, 4096], P('wshard')
- grad_w_up: float32 [1536, 4096], P('wshard')
- grad_w_down: float32 [4096, 1536], P('wshard')
Inputs may be any that keep to these rules, and one draw needn't show every extreme that they name: Each sequence has 1024 slots of which the first lengths[s] are valid; in every draw one sequence is full and one has exactly 256 valid slots.
All inputs are finite; a program needn't handle non-finite values.
Results may differ from a plain program's by a relative error of at most 0.014.
Values may be sent and summed in bfloat16 or wider, within the bound.
A program may use at most 320 MiB of HBM per device.

v0:
```python
import jax
import jax.numpy as jnp
from jax import lax
from jax.sharding import PartitionSpec as P

EPS = 1e-06
NEG_FILL = -1e30
BF16 = jnp.bfloat16
F32 = jnp.float32


def product(left, right):
    return jnp.dot(left, right, preferred_element_type=F32)


def product_tn(left, right):
    return lax.dot_general(left, right, (((0,), (0,)), ((), ())), preferred_element_type=F32)


def product_nt(left, right):
    return lax.dot_general(left, right, (((1,), (1,)), ((), ())), preferred_element_type=F32)


def rms_norm(values, gain):
    return values * lax.rsqrt(jnp.mean(values * values, axis=-1, keepdims=True) + EPS) * gain


def gate_product(attended, gate_pre):
    return attended * jax.nn.sigmoid(gate_pre)


def swiglu(gate, upward):
    return jax.nn.silu(gate) * upward


def gather_rows(shard):
    return lax.all_gather(shard, "wshard", axis=0, tiled=True)


def scatter_rows(partial):
    return lax.psum_scatter(partial.astype(BF16), "wshard", scatter_dimension=0, tiled=True)


def gather_slots(shard):
    return lax.all_gather(shard, "seq", axis=0, tiled=True)


def scatter_slots(partial):
    return lax.psum_scatter(partial.astype(BF16), "seq", scatter_dimension=0, tiled=True).astype(
        F32
    )


def share_columns(share):
    return lax.all_gather(share, "seq", axis=1, tiled=True).astype(F32)


def block_scores(query_block, key_block, cum_rows, cum_keys, first_row, length, scale):
    plain = jnp.einsum("qhd,khd->hqk", query_block, key_block, preferred_element_type=F32) * scale
    plain = plain + cum_rows.T[:, :, None] - cum_keys.T[:, None, :]
    rows = first_row + jnp.arange(query_block.shape[0], dtype=jnp.int32)
    columns = jnp.arange(key_block.shape[0], dtype=jnp.int32)
    allowed = (columns[None, :] <= rows[:, None]) & (columns[None, :] < length)
    return jnp.where(allowed[None], plain, NEG_FILL)


def attention_forward(query, key, value, cumulative, length, scale, block):
    slots = query.shape[0]
    blocks = []
    log_totals = []
    for first in range(0, slots, block):
        last = first + block
        masked = block_scores(
            query[first:last],
            key[:last],
            cumulative[first:last],
            cumulative[:last],
            first,
            length,
            scale,
        )
        log_total = jax.nn.logsumexp(masked, axis=-1, keepdims=True)
        probability = jnp.exp(masked - log_total).astype(BF16)
        blocks.append(
            jnp.einsum("hqk,khd->qhd", probability, value[:last], preferred_element_type=F32)
        )
        log_totals.append(log_total)
    return (jnp.concatenate(blocks, axis=0).astype(BF16), log_totals)


def attention_backward(query, key, value, grad, cumulative, log_totals, length, scale, block):
    slots, heads, size = query.shape
    grad_query = []
    grad_key = jnp.zeros((slots, heads, size), F32)
    grad_value = jnp.zeros((slots, heads, size), F32)
    grad_cum = jnp.zeros((slots, heads), F32)
    for number, first in enumerate(range(0, slots, block)):
        last = first + block
        masked = block_scores(
            query[first:last],
            key[:last],
            cumulative[first:last],
            cumulative[:last],
            first,
            length,
            scale,
        )
        probability = jnp.exp(masked - log_totals[number])
        probability_low = probability.astype(BF16)
        grad_block = grad[first:last]
        grad_probability = jnp.einsum(
            "qhd,khd->hqk", grad_block, value[:last], preferred_element_type=F32
        )
        row_dot = jnp.sum(grad_probability * probability, axis=-1, keepdims=True)
        score_terms = probability * (grad_probability - row_dot)
        grad_scores = score_terms.astype(BF16)
        grad_cum = grad_cum.at[first:last].add(jnp.sum(score_terms, axis=2).T)
        grad_cum = grad_cum.at[:last].add(-jnp.sum(score_terms, axis=1).T)
        grad_query.append(
            jnp.einsum("hqk,khd->qhd", grad_scores, key[:last], preferred_element_type=F32)
        )
        grad_key = grad_key.at[:last].add(
            jnp.einsum("hqk,qhd->khd", grad_scores, query[first:last], preferred_element_type=F32)
        )
        grad_value = grad_value.at[:last].add(
            jnp.einsum("hqk,qhd->khd", probability_low, grad_block, preferred_element_type=F32)
        )
    grad_query = (jnp.concatenate(grad_query, axis=0) * scale).astype(BF16)
    return (grad_query, (grad_key * scale).astype(BF16), grad_value.astype(BF16), grad_cum)


def on_device(
    layer_input,
    lengths,
    norm_attn,
    w_query,
    w_key,
    w_value,
    w_ogate,
    w_forget,
    forget_bias,
    w_out,
    norm_ffn,
    w_gate,
    w_up,
    w_down,
    output_grad,
):
    tokens, width = layer_input.shape[1:]
    heads = forget_bias.shape[0]
    groups = lax.axis_size("seq")
    owners = lax.axis_size("wshard")
    local_heads = heads // groups
    head_size = width // heads
    slots = tokens * groups
    part = width // groups
    units = w_gate.shape[1]
    own_units = units // owners
    piece = own_units // groups
    local_units = units // groups
    block = min(512, slots)
    scale = head_size ** (-0.5)
    length = lengths[0]
    rank = lax.axis_index("seq")
    positions = rank * tokens + jnp.arange(tokens, dtype=jnp.int32)
    valid_slots = (positions < length).astype(F32)[:, None]
    inputs = layer_input[0].astype(F32)
    cotangent = output_grad[0].astype(F32) * valid_slots

    def columns(weight):
        return lax.dynamic_slice_in_dim(weight, rank * part, part, 1)

    def unit_columns(weight):
        cut = lax.dynamic_index_in_dim(
            weight.reshape(-1, owners, groups, piece), rank, 2, keepdims=False
        )
        return cut.reshape(-1, local_units)

    pad = -local_heads % 128
    forget_columns = jnp.pad(
        lax.dynamic_slice_in_dim(w_forget, rank * local_heads, local_heads, 1), ((0, 0), (0, pad))
    )
    normed_attn = gather_slots(rms_norm(inputs, norm_attn).astype(BF16))
    full_attn = gather_rows(
        jnp.concatenate(
            [columns(w_query), columns(w_key), columns(w_value), columns(w_ogate), forget_columns],
            axis=1,
        )
    )
    cut_out = gather_rows(columns(w_out))
    full_out = lax.all_to_all(cut_out, "seq", split_axis=0, concat_axis=1, tiled=True)
    full_gate_up = gather_rows(jnp.concatenate([unit_columns(w_gate), unit_columns(w_up)], axis=1))
    full_down = gather_rows(lax.dynamic_slice_in_dim(w_down, rank * piece, piece, 0))
    cotangent_low = gather_slots(cotangent.astype(BF16))
    query = product(normed_attn, full_attn[:, :part]).astype(BF16)
    key = product(normed_attn, full_attn[:, part : 2 * part]).astype(BF16)
    value = product(normed_attn, full_attn[:, 2 * part : 3 * part]).astype(BF16)
    gate_pre = product(normed_attn, full_attn[:, 3 * part : 4 * part])
    forget_pre = product(normed_attn, full_attn[:, 4 * part :])[:, :local_heads].astype(BF16)
    query = query.reshape(slots, local_heads, head_size)
    key = key.reshape(slots, local_heads, head_size)
    value = value.reshape(slots, local_heads, head_size)
    bias_local = lax.dynamic_slice_in_dim(forget_bias, rank * local_heads, local_heads)
    forget_total = forget_pre.astype(F32) + bias_local
    log_forget, pull_forget = jax.vjp(jax.nn.log_sigmoid, forget_total)
    cumulative = jnp.cumsum(log_forget, axis=0)
    head_output, log_totals = attention_forward(query, key, value, cumulative, length, scale, block)
    attended = head_output.reshape(slots, part).astype(F32)
    gated_full, pull_gate = jax.vjp(gate_product, attended, gate_pre)
    gated = gated_full.astype(BF16)
    middle = inputs + scatter_slots(product(gated, full_out))
    normed_ffn_full, pull_ffn_norm = jax.vjp(rms_norm, middle, norm_ffn)
    normed_ffn = gather_slots(normed_ffn_full.astype(BF16))
    gate_value = product(normed_ffn, full_gate_up[:, :local_units])
    up_value = product(normed_ffn, full_gate_up[:, local_units:])
    hidden_full, pull_swiglu = jax.vjp(swiglu, gate_value, up_value)
    hidden = hidden_full.astype(BF16)
    result = middle + scatter_slots(product(hidden, full_down))
    layer_output = result.astype(BF16)[None]
    grad_hidden = product_nt(cotangent_low, full_down)
    grad_gate_full, grad_up_full = pull_swiglu(grad_hidden)
    grad_gate_up = jnp.concatenate([grad_gate_full.astype(BF16), grad_up_full.astype(BF16)], axis=1)
    grad_normed_ffn = scatter_slots(product_nt(grad_gate_up, full_gate_up))
    share_down = scatter_rows(product_tn(hidden, cotangent_low))
    share_gate_up = scatter_rows(product_tn(normed_ffn, grad_gate_up))
    grad_middle_part, grad_norm_ffn = pull_ffn_norm(grad_normed_ffn)
    grad_middle = cotangent + grad_middle_part
    grad_branch = gather_slots(grad_middle.astype(BF16))
    grad_gated = product_nt(grad_branch, full_out)
    grad_w_out = product_tn(gated, grad_branch).astype(BF16)
    share_out = scatter_rows(
        lax.all_to_all(grad_w_out, "seq", split_axis=1, concat_axis=0, tiled=True)
    )
    grad_attended_full, grad_gate_pre_full = pull_gate(grad_gated)
    grad_attended = grad_attended_full.astype(BF16).reshape(slots, local_heads, head_size)
    grad_gate_pre = grad_gate_pre_full.astype(BF16)
    grad_query, grad_key, grad_value, grad_cum = attention_backward(
        query, key, value, grad_attended, cumulative, log_totals, length, scale, block
    )
    grad_log_forget = jnp.flip(jnp.cumsum(jnp.flip(grad_cum, 0), axis=0), 0)
    grad_forget_total = pull_forget(grad_log_forget)[0]
    grad_bias_local = jnp.sum(grad_forget_total, axis=0)
    grad_bias = lax.dynamic_update_slice_in_dim(
        jnp.zeros((heads,), F32), grad_bias_local, rank * local_heads, 0
    )
    grad_attn = jnp.concatenate(
        [
            grad_query.reshape(slots, part),
            grad_key.reshape(slots, part),
            grad_value.reshape(slots, part),
            grad_gate_pre,
            jnp.pad(grad_forget_total.astype(BF16), ((0, 0), (0, pad))),
        ],
        axis=1,
    )
    grad_normed_attn = scatter_slots(product_nt(grad_attn, full_attn))
    share_attn = scatter_rows(product_tn(normed_attn, grad_attn))
    unused_normed, pull_attn_norm = jax.vjp(rms_norm, inputs, norm_attn)
    grad_input_part, grad_norm_attn = pull_attn_norm(grad_normed_attn)
    grad_input = (grad_middle + grad_input_part)[None]
    rows = w_query.shape[0]
    all_down = lax.all_gather(share_down, "seq", axis=0, tiled=True).astype(F32)
    all_gate_up = lax.all_gather(share_gate_up, "seq", axis=0, tiled=False)
    all_gate_up = all_gate_up.reshape(groups, rows, 2, owners, piece).transpose(2, 1, 3, 0, 4)
    all_gate_up = all_gate_up.reshape(2, rows, units).astype(F32)
    all_out = share_columns(share_out)
    all_attn = lax.all_gather(share_attn, "seq", axis=0, tiled=False)

    def whole(first, size):
        cut = all_attn[:, :, first : first + size].transpose(1, 0, 2)
        return cut.reshape(rows, groups * size).astype(F32)

    small = lax.psum((grad_norm_attn, grad_norm_ffn, grad_bias), ("seq", "wshard"))
    return (
        layer_output,
        grad_input,
        small[0],
        whole(0, part),
        whole(part, part),
        whole(2 * part, part),
        whole(3 * part, part),
        whole(4 * part, local_heads),
        small[2],
        all_out,
        small[1],
        all_gate_up[0],
        all_gate_up[1],
        all_down,
    )


def solution(mesh):
    rows = P("wshard", None)
    slots = P("wshard", "seq", None)
    return jax.shard_map(
        on_device,
        mesh=mesh,
        in_specs=(
            slots,
            P("wshard"),
            P(),
            rows,
            rows,
            rows,
            rows,
            rows,
            P(),
            rows,
            P(),
            rows,
            rows,
            rows,
            slots,
        ),
        out_specs=(
            slots,
            slots,
            P(),
            rows,
            rows,
            rows,
            rows,
            rows,
            P(),
            rows,
            P(),
            rows,
            rows,
            rows,
        ),
        check_vma=False,
    )
```

profile of v0, /device:TPU:0, one launch (start us, length us, event | category | flops | bytes accessed | tf_op | source)
XLA Modules:
  0.0 979.0 jit_solution(494081339802589565)
XLA Ops:
  19.4 16.4 %all-gather.18.cloned.1.call-done = bf16[1536,384]{1,0:T(8,128)(2,1)} async-done(((bf16[192,384]{1,0:T(8,128)(2,1)}), bf16[1536,384]{1,0:T(8,128)(2,1)}) %all-gather.18.cloned.1.call-update) | async-done | bytes 1179664 | tf_op jit(solution)/shard_map/all_gather | solution.py:37
  35.8 3.5 all-to-all-start
  41.4 21.1 %all-to-all-done = bf16[4,384,384]{2,1,0:T(8,128)(2,1)S(1)} async-done(((bf16[4,384,384]{2,1,0:T(8,128)(2,1)}), bf16[4,384,384]{2,1,0:T(8,128)(2,1)S(1)}, u32[]{:S(2)}, u32[]{:S(2)}) %all-to-all-start) | async-done | bytes 1179680 | tf_op jit(solution)/shard_map/all_to_all | solution.py:191
  64.0 23.1 %all-gather.14.cloned.1.call-done = bf16[1024,1536]{1,0:T(8,128)(2,1)} async-done(((bf16[256,1536]{1,0:T(8,128)(2,1)}), bf16[1024,1536]{1,0:T(8,128)(2,1)}) %all-gather.14.cloned.1.call-update) | async-done | bytes 3145744 | tf_op jit(solution)/shard_map/all_gather | solution.py:45
  87.0 57.1 %all-gather.16.cloned.1.call-done = bf16[1536,1664]{1,0:T(8,128)(2,1)} async-done(((bf16[192,1664]{1,0:T(8,128)(2,1)}), bf16[1536,1664]{1,0:T(8,128)(2,1)}) %all-gather.16.cloned.1.call-update) | async-done | bytes 5111824 | tf_op jit(solution)/shard_map/all_gather | solution.py:37
  144.2 3.1 fusion.64
  150.3 3.8 convolution_convert_fusion.8
  154.1 3.1 convolution_convert_fusion.10
  157.3 2.8 convolution_convert_fusion.9
  163.4 3.6 fusion.86
  167.0 2.8 exponential_reduce_fusion
  171.5 2.3 fusion.51
  173.9 3.1 add_divide_fusion.1
  178.1 3.5 convolution_convert_fusion.4
  184.8 4.1 reshape.507
  188.9 2.3 reshape.509
  191.2 6.7 dynamic-slice_reduce_fusion
  199.1 25.4 %reduce-scatter.9.cloned.1.call-done = bf16[256,1536]{1,0:T(8,128)(2,1)} async-done(((bf16[1024,1536]{1,0:T(8,128)(2,1)}), bf16[256,1536]{1,0:T(8,128)(2,1)}) %reduce-scatter.9.cloned.1.call-update) | async-done | bytes 786448 | tf_op jit(solution)/shard_map/reduce_scatter | solution.py:49
  228.6 42.0 %all-gather.26.cloned.1.call-done = bf16[1024,1536]{1,0:T(8,128)(2,1)} async-done(((bf16[256,1536]{1,0:T(8,128)(2,1)}), bf16[1024,1536]{1,0:T(8,128)(2,1)}) %all-gather.26.cloned.1.call-update) | async-done | bytes 3145744 | tf_op jit(solution)/shard_map/all_gather | solution.py:45
  270.7 40.3 %all-gather.24.cloned.1.call-done = bf16[1024,1536]{1,0:T(8,128)(2,1)} async-done(((bf16[128,1536]{1,0:T(8,128)(2,1)}), bf16[1024,1536]{1,0:T(8,128)(2,1)}) %all-gather.24.cloned.1.call-update) | async-done | bytes 3145744 | tf_op jit(solution)/shard_map/all_gather | solution.py:37
  311.0 8.2 fusion.88
  319.2 57.6 %all-gather.22.cloned.1.call-done = bf16[1536,2048]{1,0:T(8,128)(2,1)} async-done(((bf16[192,2048]{1,0:T(8,128)(2,1)}), bf16[1536,2048]{1,0:T(8,128)(2,1)}) %all-gather.22.cloned.1.call-update) | async-done | bytes 6291472 | tf_op jit(solution)/shard_map/all_gather | solution.py:37
  376.8 44.9 %all-gather.20.cloned.1.call-done = bf16[1024,1536]{1,0:T(8,128)(2,1)} async-done(((bf16[256,1536]{1,0:T(8,128)(2,1)}), bf16[1024,1536]{1,0:T(8,128)(2,1)}) %all-gather.20.cloned.1.call-update) | async-done | bytes 3145744 | tf_op jit(solution)/shard_map/all_gather | solution.py:45
  421.8 8.5 fusion.6
  430.3 8.5 fusion.4
  440.1 9.4 convolution_convert_fusion.2
  450.0 43.6 %reduce-scatter.13.cloned.1.call-done = bf16[256,1536]{1,0:T(8,128)(2,1)} async-done(((bf16[1024,1536]{1,0:T(8,128)(2,1)}), bf16[256,1536]{1,0:T(8,128)(2,1)}) %reduce-scatter.13.cloned.1.call-update) | async-done | bytes 786448 | tf_op jit(solution)/shard_map/reduce_scatter | solution.py:49
  493.6 2.4 fusion.28
  496.0 2.7 fusion.78
  498.8 7.6 convolution_convert_fusion.5
  506.5 11.6 %convolution_convert_fusion.1 = bf16[1536,2048]{1,0:T(8,128)(2,1)} fusion(bf16[1024,1536]{1,0:T(8,128)(2,1)} %all-gather.20.cloned.1.call-done, bf16[1024,1024]{0,1:T(8,128)(2,1)} %get-tuple-element.150, bf16[1024,1024]{0,1:T(8,128)(2,1)} %copy-done.58), kind=kOutput, calls=%fused_computation.7 | convolution fusion | flops 6453985280 | bytes 13631488 | tf_op jit(solution)/shard_map/dot_general | solution.py:17
  518.2 24.6 %all-gather.28.cloned.1.call-done = bf16[1024,1536]{1,0:T(8,128)(2,1)} async-done(((bf16[256,1536]{1,0:T(8,128)(2,1)}), bf16[1024,1536]{1,0:T(8,128)(2,1)}) %all-gather.28.cloned.1.call-update) | async-done | bytes 3145744 | tf_op jit(solution)/shard_map/all_gather | solution.py:45
  542.7 5.3 multiply_convert_fusion.2
  548.8 4.6 multiply_reduce_fusion.1
  553.4 5.2 fusion.80
  558.7 4.4 multiply_reduce_fusion
  563.1 5.7 fusion.79
  571.6 2.7 rev.8
  574.3 2.8 fusion.42
  577.2 5.3 fusion.12
  588.9 2.4 fusion.37
  594.7 7.9 convolution_convert_fusion
  603.3 3.8 convolution_convert_fusion.7
  607.3 18.7 %all_to_all.38 = bf16[384,4,384]{2,0,1:T(8,128)(2,1)} all-to-all(bf16[384,4,384]{2,0,1:T(8,128)(2,1)S(1)} %bitcast.215), channel_id=1, replica_groups=mesh['seq'=4,'wshard'=8] {'seq'}, dimensions={1} | all-to-all | bytes 2359296 | tf_op jit(solution)/shard_map/all_to_all | solution.py:232
  626.0 31.2 %reduce-scatter.21.cloned.1.call-done = bf16[192,2048]{1,0:T(8,128)(2,1)} async-done(((bf16[1536,2048]{1,0:T(8,128)(2,1)}), bf16[192,2048]{1,0:T(8,128)(2,1)}) %reduce-scatter.21.cloned.1.call-update) | async-done | bytes 786448 | tf_op jit(solution)/shard_map/reduce_scatter | solution.py:41
  657.3 10.2 %convolution_convert_fusion.3 = bf16[1024,1536]{1,0:T(8,128)(2,1)} fusion(bf16[1024,1664]{0,1:T(8,128)(2,1)} %copy-done.36, bf16[1536,1664]{1,0:T(8,128)(2,1)} %all-gather.16.cloned.1.call-done), kind=kOutput, calls=%fused_computation.25 | convolution fusion | flops 5236064256 | bytes 11665408 | tf_op jit(solution)/shard_map/dot_general | solution.py:21
  667.5 7.7 convolution_convert_fusion.6
  675.3 41.0 %reduce-scatter.17.cloned.1.call-done = bf16[192,1664]{1,0:T(8,128)(2,1)} async-done(((bf16[1536,1664]{1,0:T(8,128)(2,1)}), bf16[192,1664]{1,0:T(8,128)(2,1)}) %reduce-scatter.17.cloned.1.call-update) | async-done | bytes 638992 | tf_op jit(solution)/shard_map/reduce_scatter | solution.py:41
  716.3 31.0 %all-gather.30.cloned.1.call-done = bf16[512,1536]{1,0:T(8,128)(2,1)} async-done(((bf16[128,1536]{1,0:T(8,128)(2,1)}), bf16[512,1536]{1,0:T(8,128)(2,1)}) %all-gather.30.cloned.1.call-update) | async-done | bytes 1572880 | tf_op jit(solution)/shard_map/all_gather | solution.py:262
  747.4 3.5 convert_element_type.258
  750.9 31.5 %reduce-scatter.19.cloned.1.call-done = bf16[192,384]{1,0:T(8,128)(2,1)} async-done(((bf16[1536,384]{1,0:T(8,128)(2,1)}), bf16[192,384]{1,0:T(8,128)(2,1)}) %reduce-scatter.19.cloned.1.call-update) | async-done | bytes 147472 | tf_op jit(solution)/shard_map/reduce_scatter | solution.py:41
  782.5 14.6 %all_gather.52 = bf16[192,1536]{1,0:T(8,128)(2,1)S(1)} all-gather(bf16[192,384]{1,0:T(8,128)(2,1)} %reduce-scatter.19.cloned.1.call-done), channel_id=1, replica_groups=mesh['seq'=4,'wshard'=8] {'seq'}, dimensions={1}, use_global_device_ids=true | all-gather | bytes 737280 | tf_op jit(solution)/shard_map/all_gather | solution.py:55
  798.3 28.1 %all-gather.34.cloned.1.call-done = bf16[768,2048]{1,0:T(8,128)(2,1)} async-done(((bf16[192,2048]{1,0:T(8,128)(2,1)}), bf16[768,2048]{1,0:T(8,128)(2,1)}) %all-gather.34.cloned.1.call-update) | async-done | bytes 3145744 | tf_op jit(solution)/shard_map/all_gather | solution.py:263
  826.4 2.7 convert_bitcast_fusion
  832.7 3.8 copy.88
  836.4 5.0 squeeze.16
  841.5 5.7 copy.87
  847.2 5.3 squeeze.15
  852.5 20.6 %reduce-scatter.15.cloned.1.call-done = bf16[256,1536]{1,0:T(8,128)(2,1)} async-done(((bf16[1024,1536]{1,0:T(8,128)(2,1)}), bf16[256,1536]{1,0:T(8,128)(2,1)}) %reduce-scatter.15.cloned.1.call-update) | async-done | bytes 786448 | tf_op jit(solution)/shard_map/reduce_scatter | solution.py:49
  875.0 40.3 %all-reduce.5 = (f32[1536]{0:T(1024)}, f32[24]{0:T(128)}, f32[1536]{0:T(1024)}) all-reduce(f32[1536]{0:T(1024)S(1)} %get-tuple-element.140, f32[24]{0:T(128)S(1)} %negate_dynamic-update-slice_fusion, f32[1536]{0:T(1024)S(1)} %copy-done.41), channel_id=1, replica_groups=mesh['seq'=4,'wshard'=8] {'seq','wshard'}, use_global_device_ids=true, to_apply=%region_23.24 | all-reduce | flops 3096 | bytes 24768 | tf_op jit(solution)/shard_map/psum | solution.py:273
  915.4 5.4 reduce-scatter.11.cloned.1.call-done
  920.7 4.0 fusion.32
  924.7 36.9 %all-gather.32.cloned.1.call-done = bf16[768,1664]{1,0:T(8,128)(2,1)} async-done(((bf16[192,1664]{1,0:T(8,128)(2,1)}), bf16[768,1664]{1,0:T(8,128)(2,1)}) %all-gather.32.cloned.1.call-update) | async-done | bytes 2555920 | tf_op jit(solution)/shard_map/all_gather | solution.py:267
  962.5 3.5 convert_bitcast_fusion.1
  (265 shorter events, 61.9 us)
Async XLA Ops:
  7.2 176.7 %copy-start = (bf16[512,1536]{1,0:T(8,128)(2,1)S(1)}, bf16[512,1536]{1,0:T(8,128)(2,1)}, u32[]{:S(2)}) copy-start(bf16[512,1536]{1,0:T(8,128)(2,1)} %param.50) | copy-start | bytes 4718596
  7.2 28.6 %all-gather.18.cloned.1.call-start = ((), (), s32[]{:S(2)}) async-start(), calls=%async_computation.12 | async-start | bytes 1327104 | tf_op jit(solution)/shard_map/all_gather | solution.py:37
  9.0 78.1 %all-gather.14.cloned.1.call-start = ((), (), s32[]{:S(2)}) async-start(), calls=%async_computation.10 | async-start | bytes 3932160 | tf_op jit(solution)/shard_map/all_gather | solution.py:45
  11.5 28.5 %copy-start.56 = (f32[24]{0:T(128)S(1)}, f32[24]{0:T(128)}, u32[]{:S(2)}) copy-start(f32[24]{0:T(128)} %param.45) | copy-start | bytes 292
  13.8 130.4 %all-gather.16.cloned.1.call-start = ((), (), s32[]{:S(2)}) async-start(), calls=%async_computation.11 | async-start | bytes 5750784 | tf_op jit(solution)/shard_map/all_gather | solution.py:37
  35.8 26.8 %all-to-all-start = ((bf16[4,384,384]{2,1,0:T(8,128)(2,1)}), bf16[4,384,384]{2,1,0:T(8,128)(2,1)S(1)}, u32[]{:S(2)}, u32[]{:S(2)}) async-start(bf16[4,384,384]{2,1,0:T(8,128)(2,1)} %bitcast.248), calls=%async_computation | async-start | bytes 2359296 | tf_op jit(solution)/shard_map/all_to_all | solution.py:191
  39.3 185.2 %reduce-scatter.9.cloned.1.call-start = ((), (), s32[]{:S(2)}) async-start(), calls=%async_computation.13 | async-start | bytes 3932160 | tf_op jit(solution)/shard_map/reduce_scatter | solution.py:49
  40.1 107.2 %copy-start.52 = (f32[6]{0:T(128)}, f32[6]{0:T(128)S(1)}, u32[]{:S(2)}) copy-start(f32[6]{0:T(128)S(1)} %dynamic_slice.36) | copy-start | bytes 76
  150.3 3.9 copy-start.17
  154.1 8.9 copy-start.21
  154.1 6.1 copy-start.27
  157.3 12.6 %copy-start.15 = (bf16[512,384]{0,1:T(8,128)(2,1)}, bf16[512,384]{0,1:T(8,128)(2,1)S(1)}, u32[]{:S(2)}) copy-start(bf16[512,384]{0,1:T(8,128)(2,1)S(1)} %slice.294) | copy-start | bytes 1179652
  162.0 7.9 copy-start.3
  162.9 7.0 copy-start.32
  167.0 4.5 copy-start.2
  171.0 6.0 copy-start.22
  173.9 4.2 copy-start.14
  181.7 89.0 %all-gather.26.cloned.1.call-start = ((), (), s32[]{:S(2)}) async-start(), calls=%async_computation.18 | async-start | bytes 3932160 | tf_op jit(solution)/shard_map/all_gather | solution.py:45
  182.8 313.2 %copy-start.46 = (f32[256]{0:T(256)}, f32[256]{0:T(256)S(1)}, u32[]{:S(2)}) copy-start(f32[256]{0:T(256)S(1)} %compare_convert_fusion) | copy-start | bytes 3076
  183.9 127.1 %all-gather.24.cloned.1.call-start = ((), (), s32[]{:S(2)}) async-start(), calls=%async_computation.16 | async-start | bytes 3538944 | tf_op jit(solution)/shard_map/all_gather | solution.py:37
  184.7 4.2 copy-start.24
  184.7 192.1 %all-gather.22.cloned.1.call-start = ((), (), s32[]{:S(2)}) async-start(), calls=%async_computation.15 | async-start | bytes 7077888 | tf_op jit(solution)/shard_map/all_gather | solution.py:37
  191.2 33.3 %copy-start.4 = (bf16[1,256,1536]{2,1,0:T(8,128)(2,1)S(1)}, bf16[1,256,1536]{2,1,0:T(8,128)(2,1)}, u32[]{:S(2)}) copy-start(bf16[1,256,1536]{2,1,0:T(8,128)(2,1)} %param.37) | copy-start | bytes 2359300
  197.9 28.1 %copy-start.37 = (f32[1536]{0:T(1024)S(1)}, f32[1536]{0:T(1024)}, u32[]{:S(2)}) copy-start(f32[1536]{0:T(1024)} %param.47) | copy-start | bytes 18436
  199.0 222.7 %all-gather.20.cloned.1.call-start = ((), (), s32[]{:S(2)}) async-start(), calls=%async_computation.14 | async-start | bytes 3932160 | tf_op jit(solution)/shard_map/all_gather | solution.py:45
  226.0 270.0 %copy-start.42 = (f32[256]{0:T(256)}, f32[256]{0:T(256)S(1)}, u32[]{:S(2)}) copy-start(f32[256]{0:T(256)S(1)} %fusion.73) | copy-start | bytes 3076
  228.4 265.2 %reduce-scatter.13.cloned.1.call-start = ((), (), s32[]{:S(2)}) async-start(), calls=%async_computation.19 | async-start | bytes 3932160 | tf_op jit(solution)/shard_map/reduce_scatter | solution.py:49
  421.8 8.5 copy-start.54
  421.8 8.5 copy-start.55
  421.8 8.5 copy-start.57
  449.5 44.1 %copy-start.6 = (bf16[256,1536]{1,0:T(8,128)(2,1)S(1)}, bf16[256,1536]{1,0:T(8,128)(2,1)}, u32[]{:S(2)}) copy-start(bf16[256,1536]{1,0:T(8,128)(2,1)} %reduce-scatter.9.cloned.1.call-done) | copy-start | bytes 2359300
  449.5 93.2 %all-gather.28.cloned.1.call-start = ((), (), s32[]{:S(2)}) async-start(), calls=%async_computation.20 | async-start | bytes 3932160 | tf_op jit(solution)/shard_map/all_gather | solution.py:45
  496.0 10.4 %copy-start.50 = (f32[256]{0:T(256)}, f32[256]{0:T(256)S(1)}, u32[]{:S(2)}) copy-start(f32[256]{0:T(256)S(1)} %multiply_multiply_fusion.1) | copy-start | bytes 3076
  498.7 104.0 %reduce-scatter.23.cloned.1.call-start = ((), (), s32[]{:S(2)}) async-start(), calls=%async_computation.25 | async-start | bytes 3538944 | tf_op jit(solution)/shard_map/reduce_scatter | solution.py:41
  506.4 150.8 %reduce-scatter.21.cloned.1.call-start = ((), (), s32[]{:S(2)}) async-start(), calls=%async_computation.24 | async-start | bytes 7077888 | tf_op jit(solution)/shard_map/reduce_scatter | solution.py:41
  518.1 198.2 %reduce-scatter.17.cloned.1.call-start = ((), (), s32[]{:S(2)}) async-start(), calls=%async_computation.22 | async-start | bytes 5750784 | tf_op jit(solution)/shard_map/reduce_scatter | solution.py:41
  548.8 4.6 copy-start.33
  548.8 9.8 %slice-start = ((s8[12582912]{0:T(1024)(128)(4,1)}), s8[4194304]{0:T(1024)(128)(4,1)S(1)}, s32[]{:S(2)}) async-start(s8[12582912]{0:T(1024)(128)(4,1)} %bitcast.202), calls=%async_computation.29 | async-start | bytes 8388608
  548.8 9.8 %slice-start.1 = ((s8[12582912]{0:T(1024)(128)(4,1)}), s8[4194304]{0:T(1024)(128)(4,1)S(1)}, s32[]{:S(2)}) async-start(s8[12582912]{0:T(1024)(128)(4,1)} %bitcast.202), calls=%async_computation.30 | async-start | bytes 8388608
  553.4 5.2 slice-start.2
  574.3 9.5 slice-start.8
  577.2 5.5 copy-start.5
  577.2 5.5 copy-start.26
  577.2 6.6 slice-start.9
  577.2 8.0 slice-start.6
  582.5 4.8 slice-start.3
  583.8 3.8 slice-start.4
  585.1 3.7 slice-start.5
  602.7 144.7 %all-gather.30.cloned.1.call-start = ((), (), s32[]{:S(2)}) async-start(), calls=%async_computation.26 | async-start | bytes 1966080 | tf_op jit(solution)/shard_map/all_gather | solution.py:262
  603.3 179.2 %reduce-scatter.19.cloned.1.call-start = ((), (), s32[]{:S(2)}) async-start(), calls=%async_computation.23 | async-start | bytes 1327104 | tf_op jit(solution)/shard_map/reduce_scatter | solution.py:41
  626.0 200.4 %all-gather.34.cloned.1.call-start = ((), (), s32[]{:S(2)}) async-start(), calls=%async_computation.28 | async-start | bytes 3932160 | tf_op jit(solution)/shard_map/all_gather | solution.py:263
  657.3 215.9 %reduce-scatter.15.cloned.1.call-start = ((), (), s32[]{:S(2)}) async-start(), calls=%async_computation.21 | async-start | bytes 3932160 | tf_op jit(solution)/shard_map/reduce_scatter | solution.py:49
  667.5 253.2 %reduce-scatter.11.cloned.1.call-start = ((), (), s32[]{:S(2)}) async-start(), calls=%async_computation.17 | async-start | bytes 3932160 | tf_op jit(solution)/shard_map/reduce_scatter | solution.py:49
  675.3 286.3 %all-gather.32.cloned.1.call-start = ((), (), s32[]{:S(2)}) async-start(), calls=%async_computation.27 | async-start | bytes 3194880 | tf_op jit(solution)/shard_map/all_gather | solution.py:267
  847.2 26.0 %copy-start.40 = (f32[1536]{0:T(1024)S(1)}, f32[1536]{0:T(1024)}, u32[]{:S(2)}) copy-start(f32[1536]{0:T(1024)} %param.39) | copy-start | bytes 18436
  847.2 26.0 %copy-start.45 = (f32[256]{0:T(256)S(1)}, f32[256]{0:T(256)}, u32[]{:S(2)}) copy-start(f32[256]{0:T(256)} %copy-done.44) | copy-start | bytes 3076
  847.2 27.8 %copy-start.41 = (f32[1536]{0:T(1024)S(1)}, f32[1536]{0:T(1024)}, u32[]{:S(2)}) copy-start(f32[1536]{0:T(1024)} %get-tuple-element.138) | copy-start | bytes 18436
  847.2 68.2 %copy-start.49 = (f32[256]{0:T(256)S(1)}, f32[256]{0:T(256)}, u32[]{:S(2)}) copy-start(f32[256]{0:T(256)} %copy-done.48) | copy-start | bytes 3076
  847.2 73.5 %copy-start.8 = (bf16[256,1536]{1,0:T(8,128)(2,1)S(1)}, bf16[256,1536]{1,0:T(8,128)(2,1)}, u32[]{:S(2)}) copy-start(bf16[256,1536]{1,0:T(8,128)(2,1)} %reduce-scatter.13.cloned.1.call-done) | copy-start | bytes 2359300
  847.2 73.5 %copy-start.38 = (f32[1536]{0:T(1024)S(1)}, f32[1536]{0:T(1024)}, u32[]{:S(2)}) copy-start(f32[1536]{0:T(1024)} %param.47) | copy-start | bytes 18436
  847.2 73.5 %copy-start.43 = (f32[256]{0:T(256)S(1)}, f32[256]{0:T(256)}, u32[]{:S(2)}) copy-start(f32[256]{0:T(256)} %copy-done.42) | copy-start | bytes 3076
  847.2 73.5 %copy-start.47 = (f32[256]{0:T(256)S(1)}, f32[256]{0:T(256)}, u32[]{:S(2)}) copy-start(f32[256]{0:T(256)} %copy-done.46) | copy-start | bytes 3076
  847.2 73.5 %copy-start.51 = (f32[256]{0:T(256)S(1)}, f32[256]{0:T(256)}, u32[]{:S(2)}) copy-start(f32[256]{0:T(256)} %copy-done.50) | copy-start | bytes 3076
  968.0 4.0 copy-start.1
  (25 other events, 54.5 us)
Sparse Core Ops, SparseCore 0:
  10.2 25.4 all-gather.17
  38.2 48.8 all-gather.13
  89.3 54.8 all-gather.15
  181.8 42.6 reduce-scatter.8
  226.8 43.8 all-gather.25
  272.7 38.2 all-gather.23
  313.2 63.5 all-gather.21
  379.2 42.4 all-gather.19
  449.6 43.8 reduce-scatter.12
  498.9 43.8 all-gather.27
  545.6 40.3 reduce-scatter.22
  588.2 69.0 reduce-scatter.20
  659.6 56.7 reduce-scatter.16
  718.0 29.3 all-gather.29
  749.5 32.9 reduce-scatter.18
  784.2 42.1 all-gather.33
  829.2 43.8 reduce-scatter.14
  876.0 44.6 reduce-scatter.10
  922.6 38.9 all-gather.31
where the time goes:
time: 989 us; the launch traced here: 979 us
  waiting for transfers between devices  623 us (63%)
  matrix products  140 us (14%)
  blocking collectives  73.7 us (7%)
  local copies, waits for them, and re-layouts  68.5 us (7%)
  other arithmetic  53.1 us (5%)
  between operations  16.2 us (2%)
    all_gather x4, waiting for transfers between devices, gather_rows(): return lax.all_gather(shard, 'wshard', axis=0, tiled=True)  171 us
    all_gather x4, waiting for transfers between devices, gather_slots(): return lax.all_gather(shard, 'seq', axis=0, tiled=True)  135 us
    reduce_scatter x4, waiting for transfers between devices, scatter_rows(): lax.psum_scatter(partial.astype(BF16), 'wshard', scatter_dimension=0, til...  104 us
    reduce_scatter x4, waiting for transfers between devices, scatter_slots(): lax.psum_scatter(partial.astype(BF16), 'seq', scatter_dimension=0, tiled=...  95.1 us
    dot_general x9, matrix products, product(): return jnp.dot(left, right, preferred_element_type=F32)  44.1 us
    psum x1, blocking collectives, on_device(): lax.psum((grad_norm_attn, grad_norm_ffn, grad_bias), ('seq', 'wshard'))  40.3 us
    all_gather x1, waiting for transfers between devices, on_device(): all_attn = lax.all_gather(share_attn, 'seq', axis=0, tiled=False)  36.9 us
    dot_general x4, matrix products, product_nt(): lax.dot_general(left, right, (((1,), (1,)), ((), ())), preferred_element_...  33.1 us
  transfers between devices with their start and end apart: 20, of which 19 were waited for; matrix products, arithmetic and copies ran while one was open for 18% of the time, Pallas kernels for 0%

commit v1 on v0

--- a/solution.py
+++ b/solution.py
@@ -2,6 +2,7 @@
 import jax.numpy as jnp
 from jax import lax
 from jax.sharding import PartitionSpec as P
+from jax.lax import all_to_all, axis_size
 
 EPS = 1e-06
 NEG_FILL = -1e30
@@ -188,7 +189,15 @@
         )
     )
     cut_out = gather_rows(columns(w_out))
-    full_out = lax.all_to_all(cut_out, "seq", split_axis=0, concat_axis=1, tiled=True)
+
+    def prepare_teams(xin, along_axis):
+        earlier = jnp.concatenate(
+            all_to_all(jnp.stack(jnp.split(xin, axis_size(along_axis), axis=0)), along_axis, 0, 0),
+            axis=1,
+        )
+        return earlier
+
+    full_out = prepare_teams(cut_out, "seq")
     full_gate_up = gather_rows(jnp.concatenate([unit_columns(w_gate), unit_columns(w_up)], axis=1))
     full_down = gather_rows(lax.dynamic_slice_in_dim(w_down, rank * piece, piece, 0))
     cotangent_low = gather_slots(cotangent.astype(BF16))

time: 989 us -> 989 us (level)
    all_gather x4, waiting for transfers between devices: 135 us -> 159 us  [gather_slots(): return lax.all_gather(shard, 'seq', axis=0, tiled=True)]
    all_to_all x1, waiting for transfers between devices: 21.1 us -> 0.01 us  [prepare_teams(): all_to_all(jnp.stack(jnp.split(xin, axis_size(along_axis), axis=0)), alon...]
  transfers between devices with their start and end apart: 20 -> 20, of which waited for: 19 -> 18; matrix products, arithmetic and copies ran while one was open for 18% -> 21% of each run, Pallas kernels for 0% -> 0%
where the time goes in v1:
time: 989 us; the launch traced here: 984 us
  waiting for transfers between devices  624 us (63%)
  matrix products  142 us (14%)
  blocking collectives  73.5 us (7%)
  local copies, waits for them, and re-layouts  67.6 us (7%)
  other arithmetic  54.6 us (6%)
  between operations  16 us (2%)
    all_gather x4, waiting for transfers between devices, gather_rows(): return lax.all_gather(shard, 'wshard', axis=0, tiled=True)  169 us
    all_gather x4, waiting for transfers between devices, gather_slots(): return lax.all_gather(shard, 'seq', axis=0, tiled=True)  159 us
    reduce_scatter x4, waiting for transfers between devices, scatter_rows(): lax.psum_scatter(partial.astype(BF16), 'wshard', scatter_dimension=0, til...  104 us
    reduce_scatter x4, waiting for transfers between devices, scatter_slots(): lax.psum_scatter(partial.astype(BF16), 'seq', scatter_dimension=0, tiled=...  95.3 us
    dot_general x9, matrix products, product(): return jnp.dot(left, right, preferred_element_type=F32)  45.8 us
    psum x1, blocking collectives, on_device(): lax.psum((grad_norm_attn, grad_norm_ffn, grad_bias), ('seq', 'wshard'))  40.3 us
    all_gather x1, waiting for transfers between devices, on_device(): all_attn = lax.all_gather(share_attn, 'seq', axis=0, tiled=False)  36.9 us
    dot_general x4, matrix products, product_nt(): lax.dot_general(left, right, (((1,), (1,)), ((), ())), preferred_element_...  33.1 us
  transfers between devices with their start and end apart: 20, of which 18 were waited for; matrix products, arithmetic and copies ran while one was open for 21% of the time, Pallas kernels for 0%

profile of v1, /device:TPU:0, one launch (start us, length us, event | category | flops | bytes accessed | tf_op | source)
XLA Modules:
  0.0 984.1 jit_solution(9195829652803567938)
XLA Ops:
  21.5 14.3 %all-gather.18.cloned.1.call-done = bf16[1536,384]{1,0:T(8,128)(2,1)} async-done(((bf16[192,384]{1,0:T(8,128)(2,1)}), bf16[1536,384]{1,0:T(8,128)(2,1)}) %all-gather.18.cloned.1.call-update) | async-done | bytes 1179664 | tf_op jit(solution)/shard_map/all_gather | solution.py:38
  39.2 4.3 all-to-all-start
  43.5 47.5 %all-gather.14.cloned.1.call-done = bf16[1024,1536]{1,0:T(8,128)(2,1)} async-done(((bf16[256,1536]{1,0:T(8,128)(2,1)}), bf16[1024,1536]{1,0:T(8,128)(2,1)}) %all-gather.14.cloned.1.call-update) | async-done | bytes 3145744 | tf_op jit(solution)/shard_map/all_gather | solution.py:46
  91.1 57.1 %all-gather.16.cloned.1.call-done = bf16[1536,1664]{1,0:T(8,128)(2,1)} async-done(((bf16[192,1664]{1,0:T(8,128)(2,1)}), bf16[1536,1664]{1,0:T(8,128)(2,1)}) %all-gather.16.cloned.1.call-update) | async-done | bytes 5111824 | tf_op jit(solution)/shard_map/all_gather | solution.py:38
  148.2 3.1 fusion.64
  154.5 3.8 convolution_convert_fusion.8
  158.3 3.1 convolution_convert_fusion.10
  161.5 3.1 convolution_convert_fusion.9
  167.9 3.6 fusion.87
  172.6 2.8 exponential_reduce_fusion
  175.5 3.2 add_divide_fusion.1
  178.8 3.0 fusion.51
  181.8 4.9 convolution_convert_fusion.4
  189.9 4.1 reshape.512
  193.9 2.3 reshape.514
  196.3 6.7 dynamic-slice_reduce_fusion
  204.1 25.4 %reduce-scatter.9.cloned.1.call-done = bf16[256,1536]{1,0:T(8,128)(2,1)} async-done(((bf16[1024,1536]{1,0:T(8,128)(2,1)}), bf16[256,1536]{1,0:T(8,128)(2,1)}) %reduce-scatter.9.cloned.1.call-update) | async-done | bytes 786448 | tf_op jit(solution)/shard_map/reduce_scatter | solution.py:50
  231.1 2.3 multiply_convert_fusion.3
  233.9 41.8 %all-gather.26.cloned.1.call-done = bf16[1024,1536]{1,0:T(8,128)(2,1)} async-done(((bf16[256,1536]{1,0:T(8,128)(2,1)}), bf16[1024,1536]{1,0:T(8,128)(2,1)}) %all-gather.26.cloned.1.call-update) | async-done | bytes 3145744 | tf_op jit(solution)/shard_map/all_gather | solution.py:46
  275.7 40.3 %all-gather.24.cloned.1.call-done = bf16[1024,1536]{1,0:T(8,128)(2,1)} async-done(((bf16[128,1536]{1,0:T(8,128)(2,1)}), bf16[1024,1536]{1,0:T(8,128)(2,1)}) %all-gather.24.cloned.1.call-update) | async-done | bytes 3145744 | tf_op jit(solution)/shard_map/all_gather | solution.py:38
  316.0 8.2 fusion.89
  324.3 57.6 %all-gather.22.cloned.1.call-done = bf16[1536,2048]{1,0:T(8,128)(2,1)} async-done(((bf16[192,2048]{1,0:T(8,128)(2,1)}), bf16[1536,2048]{1,0:T(8,128)(2,1)}) %all-gather.22.cloned.1.call-update) | async-done | bytes 6291472 | tf_op jit(solution)/shard_map/all_gather | solution.py:38
  381.9 44.9 %all-gather.20.cloned.1.call-done = bf16[1024,1536]{1,0:T(8,128)(2,1)} async-done(((bf16[256,1536]{1,0:T(8,128)(2,1)}), bf16[1024,1536]{1,0:T(8,128)(2,1)}) %all-gather.20.cloned.1.call-update) | async-done | bytes 3145744 | tf_op jit(solution)/shard_map/all_gather | solution.py:46
  426.8 8.5 fusion.6
  435.3 8.5 fusion.4
  445.1 9.4 convolution_convert_fusion.2
  454.7 43.8 %reduce-scatter.13.cloned.1.call-done = bf16[256,1536]{1,0:T(8,128)(2,1)} async-done(((bf16[1024,1536]{1,0:T(8,128)(2,1)}), bf16[256,1536]{1,0:T(8,128)(2,1)}) %reduce-scatter.13.cloned.1.call-update) | async-done | bytes 786448 | tf_op jit(solution)/shard_map/reduce_scatter | solution.py:50
  498.6 2.4 fusion.28
  501.0 2.7 fusion.78
  503.8 7.6 convolution_convert_fusion.5
  511.4 11.6 %convolution_convert_fusion.1 = bf16[1536,2048]{1,0:T(8,128)(2,1)} fusion(bf16[1024,1536]{1,0:T(8,128)(2,1)} %all-gather.20.cloned.1.call-done, bf16[1024,1024]{0,1:T(8,128)(2,1)} %get-tuple-element.150, bf16[1024,1024]{0,1:T(8,128)(2,1)} %copy-done.60), kind=kOutput, calls=%fused_computation.7 | convolution fusion | flops 6453985280 | bytes 13631488 | tf_op jit(solution)/shard_map/dot_general | solution.py:18
  523.1 24.6 %all-gather.28.cloned.1.call-done = bf16[1024,1536]{1,0:T(8,128)(2,1)} async-done(((bf16[256,1536]{1,0:T(8,128)(2,1)}), bf16[1024,1536]{1,0:T(8,128)(2,1)}) %all-gather.28.cloned.1.call-update) | async-done | bytes 3145744 | tf_op jit(solution)/shard_map/all_gather | solution.py:46
  547.7 5.3 multiply_convert_fusion.2
  553.8 4.5 multiply_reduce_fusion.1
  558.4 5.2 fusion.80
  563.6 4.4 multiply_reduce_fusion
  568.1 5.8 fusion.79
  576.6 2.7 rev.8
  579.4 2.8 fusion.42
  582.3 5.3 fusion.12
  593.9 2.4 fusion.37
  599.8 8.1 convolution_convert_fusion
  608.5 3.8 convolution_convert_fusion.7
  612.5 18.7 %all_to_all.24 = bf16[384,4,384]{2,0,1:T(8,128)(2,1)} all-to-all(bf16[384,4,384]{2,0,1:T(8,128)(2,1)S(1)} %bitcast.218), channel_id=1, replica_groups=mesh['seq'=4,'wshard'=8] {'seq'}, dimensions={1} | all-to-all | bytes 2359296 | tf_op jit(solution)/shard_map/all_to_all | solution.py:241
  631.2 31.0 %reduce-scatter.21.cloned.1.call-done = bf16[192,2048]{1,0:T(8,128)(2,1)} async-done(((bf16[1536,2048]{1,0:T(8,128)(2,1)}), bf16[192,2048]{1,0:T(8,128)(2,1)}) %reduce-scatter.21.cloned.1.call-update) | async-done | bytes 786448 | tf_op jit(solution)/shard_map/reduce_scatter | solution.py:42
  662.3 10.1 %convolution_convert_fusion.3 = bf16[1024,1536]{1,0:T(8,128)(2,1)} fusion(bf16[1024,1664]{0,1:T(8,128)(2,1)} %copy-done.38, bf16[1536,1664]{1,0:T(8,128)(2,1)} %all-gather.16.cloned.1.call-done), kind=kOutput, calls=%fused_computation.25 | convolution fusion | flops 5236064256 | bytes 11665408 | tf_op jit(solution)/shard_map/dot_general | solution.py:22
  672.6 7.7 convolution_convert_fusion.6
  680.3 41.4 %reduce-scatter.17.cloned.1.call-done = bf16[192,1664]{1,0:T(8,128)(2,1)} async-done(((bf16[1536,1664]{1,0:T(8,128)(2,1)}), bf16[192,1664]{1,0:T(8,128)(2,1)}) %reduce-scatter.17.cloned.1.call-update) | async-done | bytes 638992 | tf_op jit(solution)/shard_map/reduce_scatter | solution.py:42
  721.7 31.0 %all-gather.30.cloned.1.call-done = bf16[512,1536]{1,0:T(8,128)(2,1)} async-done(((bf16[128,1536]{1,0:T(8,128)(2,1)}), bf16[512,1536]{1,0:T(8,128)(2,1)}) %all-gather.30.cloned.1.call-update) | async-done | bytes 1572880 | tf_op jit(solution)/shard_map/all_gather | solution.py:271
  752.7 3.5 convert_element_type.258
  756.3 31.5 %reduce-scatter.19.cloned.1.call-done = bf16[192,384]{1,0:T(8,128)(2,1)} async-done(((bf16[1536,384]{1,0:T(8,128)(2,1)}), bf16[192,384]{1,0:T(8,128)(2,1)}) %reduce-scatter.19.cloned.1.call-update) | async-done | bytes 147472 | tf_op jit(solution)/shard_map/reduce_scatter | solution.py:42
  787.8 14.5 %all_gather.52 = bf16[192,1536]{1,0:T(8,128)(2,1)S(1)} all-gather(bf16[192,384]{1,0:T(8,128)(2,1)} %reduce-scatter.19.cloned.1.call-done), channel_id=1, replica_groups=mesh['seq'=4,'wshard'=8] {'seq'}, dimensions={1}, use_global_device_ids=true | all-gather | bytes 737280 | tf_op jit(solution)/shard_map/all_gather | solution.py:56
  803.5 28.3 %all-gather.34.cloned.1.call-done = bf16[768,2048]{1,0:T(8,128)(2,1)} async-done(((bf16[192,2048]{1,0:T(8,128)(2,1)}), bf16[768,2048]{1,0:T(8,128)(2,1)}) %all-gather.34.cloned.1.call-update) | async-done | bytes 3145744 | tf_op jit(solution)/shard_map/all_gather | solution.py:272
  831.8 2.7 convert_bitcast_fusion
  838.0 3.8 copy.76
  841.8 5.0 squeeze.16
  846.9 5.7 copy.75
  852.6 5.3 squeeze.15
  857.9 20.6 %reduce-scatter.15.cloned.1.call-done = bf16[256,1536]{1,0:T(8,128)(2,1)} async-done(((bf16[1024,1536]{1,0:T(8,128)(2,1)}), bf16[256,1536]{1,0:T(8,128)(2,1)}) %reduce-scatter.15.cloned.1.call-update) | async-done | bytes 786448 | tf_op jit(solution)/shard_map/reduce_scatter | solution.py:50
  880.4 40.3 %all-reduce.5 = (f32[1536]{0:T(1024)}, f32[24]{0:T(128)}, f32[1536]{0:T(1024)}) all-reduce(f32[1536]{0:T(1024)S(1)} %get-tuple-element.140, f32[24]{0:T(128)S(1)} %negate_dynamic-update-slice_fusion, f32[1536]{0:T(1024)S(1)} %copy-done.43), channel_id=1, replica_groups=mesh['seq'=4,'wshard'=8] {'seq','wshard'}, use_global_device_ids=true, to_apply=%region_23.24 | all-reduce | flops 3096 | bytes 24768 | tf_op jit(solution)/shard_map/psum | solution.py:282
  920.7 5.4 reduce-scatter.11.cloned.1.call-done
  926.1 4.0 fusion.32
  930.1 36.9 %all-gather.32.cloned.1.call-done = bf16[768,1664]{1,0:T(8,128)(2,1)} async-done(((bf16[192,1664]{1,0:T(8,128)(2,1)}), bf16[768,1664]{1,0:T(8,128)(2,1)}) %all-gather.32.cloned.1.call-update) | async-done | bytes 2555920 | tf_op jit(solution)/shard_map/all_gather | solution.py:276
  967.9 3.5 convert_bitcast_fusion.1
  (274 shorter events, 60.1 us)
Async XLA Ops:
  7.2 181.8 %copy-start = (bf16[512,1536]{1,0:T(8,128)(2,1)S(1)}, bf16[512,1536]{1,0:T(8,128)(2,1)}, u32[]{:S(2)}) copy-start(bf16[512,1536]{1,0:T(8,128)(2,1)} %param.50) | copy-start | bytes 4718596
  7.2 12.8 %copy-start.58 = (f32[24]{0:T(128)S(1)}, f32[24]{0:T(128)}, u32[]{:S(2)}) copy-start(f32[24]{0:T(128)} %param.45) | copy-start | bytes 292
  7.2 28.6 %all-gather.18.cloned.1.call-start = ((), (), s32[]{:S(2)}) async-start(), calls=%async_computation.12 | async-start | bytes 1327104 | tf_op jit(solution)/shard_map/all_gather | solution.py:38
  9.0 82.1 %all-gather.14.cloned.1.call-start = ((), (), s32[]{:S(2)}) async-start(), calls=%async_computation.10 | async-start | bytes 3932160 | tf_op jit(solution)/shard_map/all_gather | solution.py:46
  13.8 134.4 %all-gather.16.cloned.1.call-start = ((), (), s32[]{:S(2)}) async-start(), calls=%async_computation.11 | async-start | bytes 5750784 | tf_op jit(solution)/shard_map/all_gather | solution.py:38
  20.1 131.2 %copy-start.54 = (f32[6]{0:T(128)}, f32[6]{0:T(128)S(1)}, u32[]{:S(2)}) copy-start(f32[6]{0:T(128)S(1)} %dynamic_slice.36) | copy-start | bytes 76
  39.2 142.6 %all-to-all-start = ((bf16[4,384,384]{1,2,0:T(8,128)(2,1)}), bf16[4,384,384]{1,2,0:T(8,128)(2,1)}, u32[]{:S(2)}, u32[]{:S(2)}) async-start(bf16[4,384,384]{1,2,0:T(8,128)(2,1)} %pad_maximum_fusion.3), calls=%async_computation | async-start | bytes 2359296 | tf_op jit(solution)/shard_map/all_to_all | solution.py:195
  43.5 186.1 %reduce-scatter.9.cloned.1.call-start = ((), (), s32[]{:S(2)}) async-start(), calls=%async_computation.13 | async-start | bytes 3932160 | tf_op jit(solution)/shard_map/reduce_scatter | solution.py:50
  158.3 9.1 copy-start.23
  158.3 6.3 copy-start.29
  161.4 17.3 %copy-start.12 = (bf16[1024,384]{0,1:T(8,128)(2,1)}, bf16[1024,384]{0,1:T(8,128)(2,1)S(1)}, u32[]{:S(2)}) copy-start(bf16[1024,384]{0,1:T(8,128)(2,1)S(1)} %convolution_convert_fusion.10) | copy-start | bytes 2359300
  161.5 10.0 %copy-start.16 = (bf16[512,384]{0,1:T(8,128)(2,1)}, bf16[512,384]{0,1:T(8,128)(2,1)S(1)}, u32[]{:S(2)}) copy-start(bf16[512,384]{0,1:T(8,128)(2,1)S(1)} %slice.294) | copy-start | bytes 1179652
  166.5 5.1 copy-start.3
  167.4 4.1 copy-start.33
  171.5 7.3 copy-start.2
  172.6 9.2 copy-start.24
  186.7 89.0 %all-gather.26.cloned.1.call-start = ((), (), s32[]{:S(2)}) async-start(), calls=%async_computation.18 | async-start | bytes 3932160 | tf_op jit(solution)/shard_map/all_gather | solution.py:46
  187.8 313.2 %copy-start.48 = (f32[256]{0:T(256)}, f32[256]{0:T(256)S(1)}, u32[]{:S(2)}) copy-start(f32[256]{0:T(256)S(1)} %compare_convert_fusion) | copy-start | bytes 3076
  188.9 127.1 %all-gather.24.cloned.1.call-start = ((), (), s32[]{:S(2)}) async-start(), calls=%async_computation.16 | async-start | bytes 3538944 | tf_op jit(solution)/shard_map/all_gather | solution.py:38
  189.8 4.2 copy-start.26
  189.8 192.1 %all-gather.22.cloned.1.call-start = ((), (), s32[]{:S(2)}) async-start(), calls=%async_computation.15 | async-start | bytes 7077888 | tf_op jit(solution)/shard_map/all_gather | solution.py:38
  196.2 33.3 %copy-start.4 = (bf16[1,256,1536]{2,1,0:T(8,128)(2,1)S(1)}, bf16[1,256,1536]{2,1,0:T(8,128)(2,1)}, u32[]{:S(2)}) copy-start(bf16[1,256,1536]{2,1,0:T(8,128)(2,1)} %param.37) | copy-start | bytes 2359300
  203.0 28.1 %copy-start.39 = (f32[1536]{0:T(1024)S(1)}, f32[1536]{0:T(1024)}, u32[]{:S(2)}) copy-start(f32[1536]{0:T(1024)} %param.47) | copy-start | bytes 18436
  204.1 222.7 %all-gather.20.cloned.1.call-start = ((), (), s32[]{:S(2)}) async-start(), calls=%async_computation.14 | async-start | bytes 3932160 | tf_op jit(solution)/shard_map/all_gather | solution.py:46
  231.1 269.9 %copy-start.44 = (f32[256]{0:T(256)}, f32[256]{0:T(256)S(1)}, u32[]{:S(2)}) copy-start(f32[256]{0:T(256)S(1)} %fusion.73) | copy-start | bytes 3076
  233.4 265.1 %reduce-scatter.13.cloned.1.call-start = ((), (), s32[]{:S(2)}) async-start(), calls=%async_computation.19 | async-start | bytes 3932160 | tf_op jit(solution)/shard_map/reduce_scatter | solution.py:50
  426.8 8.5 copy-start.56
  426.8 8.5 copy-start.57
  426.8 8.5 copy-start.59
  454.5 44.1 %copy-start.6 = (bf16[256,1536]{1,0:T(8,128)(2,1)S(1)}, bf16[256,1536]{1,0:T(8,128)(2,1)}, u32[]{:S(2)}) copy-start(bf16[256,1536]{1,0:T(8,128)(2,1)} %reduce-scatter.9.cloned.1.call-done) | copy-start | bytes 2359300
  454.5 93.2 %all-gather.28.cloned.1.call-start = ((), (), s32[]{:S(2)}) async-start(), calls=%async_computation.20 | async-start | bytes 3932160 | tf_op jit(solution)/shard_map/all_gather | solution.py:46
  501.0 10.4 %copy-start.52 = (f32[256]{0:T(256)}, f32[256]{0:T(256)S(1)}, u32[]{:S(2)}) copy-start(f32[256]{0:T(256)S(1)} %multiply_multiply_fusion.1) | copy-start | bytes 3076
  503.7 104.3 %reduce-scatter.23.cloned.1.call-start = ((), (), s32[]{:S(2)}) async-start(), calls=%async_computation.25 | async-start | bytes 3538944 | tf_op jit(solution)/shard_map/reduce_scatter | solution.py:42
  511.4 150.9 %reduce-scatter.21.cloned.1.call-start = ((), (), s32[]{:S(2)}) async-start(), calls=%async_computation.24 | async-start | bytes 7077888 | tf_op jit(solution)/shard_map/reduce_scatter | solution.py:42
  523.1 30.7 %copy-start.17 = (bf16[512,384]{0,1:T(8,128)(2,1)S(1)}, bf16[512,384]{0,1:T(8,128)(2,1)}, u32[]{:S(2)}) copy-start(bf16[512,384]{0,1:T(8,128)(2,1)} %copy-done.16) | copy-start | bytes 1179652
  523.1 30.7 %copy-start.34 = (f32[6,512]{1,0:T(8,128)S(1)}, f32[6,512]{1,0:T(8,128)}, u32[]{:S(2)}) copy-start(f32[6,512]{1,0:T(8,128)} %copy-done.33) | copy-start | bytes 36868
  523.1 198.6 %reduce-scatter.17.cloned.1.call-start = ((), (), s32[]{:S(2)}) async-start(), calls=%async_computation.22 | async-start | bytes 5750784 | tf_op jit(solution)/shard_map/reduce_scatter | solution.py:42
  553.8 4.5 copy-start.35
  553.8 9.8 slice-start
  553.8 9.8 slice-start.1
  558.4 5.3 slice-start.2
  558.4 5.3 copy-start.13
  579.4 9.5 slice-start.8
  582.2 5.5 copy-start.5
  582.2 5.5 copy-start.28
  582.2 6.6 slice-start.9
  582.3 8.0 slice-start.6
  587.6 4.8 slice-start.3
  607.9 144.8 %all-gather.30.cloned.1.call-start = ((), (), s32[]{:S(2)}) async-start(), calls=%async_computation.26 | async-start | bytes 1966080 | tf_op jit(solution)/shard_map/all_gather | solution.py:271
  608.5 179.3 %reduce-scatter.19.cloned.1.call-start = ((), (), s32[]{:S(2)}) async-start(), calls=%async_computation.23 | async-start | bytes 1327104 | tf_op jit(solution)/shard_map/reduce_scatter | solution.py:42
  631.2 200.6 %all-gather.34.cloned.1.call-start = ((), (), s32[]{:S(2)}) async-start(), calls=%async_computation.28 | async-start | bytes 3932160 | tf_op jit(solution)/shard_map/all_gather | solution.py:272
  662.3 216.2 %reduce-scatter.15.cloned.1.call-start = ((), (), s32[]{:S(2)}) async-start(), calls=%async_computation.21 | async-start | bytes 3932160 | tf_op jit(solution)/shard_map/reduce_scatter | solution.py:50
  672.5 253.6 %reduce-scatter.11.cloned.1.call-start = ((), (), s32[]{:S(2)}) async-start(), calls=%async_computation.17 | async-start | bytes 3932160 | tf_op jit(solution)/shard_map/reduce_scatter | solution.py:50
  680.3 286.7 %all-gather.32.cloned.1.call-start = ((), (), s32[]{:S(2)}) async-start(), calls=%async_computation.27 | async-start | bytes 3194880 | tf_op jit(solution)/shard_map/all_gather | solution.py:276
  852.5 26.0 %copy-start.42 = (f32[1536]{0:T(1024)S(1)}, f32[1536]{0:T(1024)}, u32[]{:S(2)}) copy-start(f32[1536]{0:T(1024)} %param.39) | copy-start | bytes 18436
  852.6 26.0 %copy-start.47 = (f32[256]{0:T(256)S(1)}, f32[256]{0:T(256)}, u32[]{:S(2)}) copy-start(f32[256]{0:T(256)} %copy-done.46) | copy-start | bytes 3076
  852.6 27.8 %copy-start.43 = (f32[1536]{0:T(1024)S(1)}, f32[1536]{0:T(1024)}, u32[]{:S(2)}) copy-start(f32[1536]{0:T(1024)} %get-tuple-element.138) | copy-start | bytes 18436
  852.6 68.2 %copy-start.51 = (f32[256]{0:T(256)S(1)}, f32[256]{0:T(256)}, u32[]{:S(2)}) copy-start(f32[256]{0:T(256)} %copy-done.50) | copy-start | bytes 3076
  852.6 73.5 %copy-start.8 = (bf16[256,1536]{1,0:T(8,128)(2,1)S(1)}, bf16[256,1536]{1,0:T(8,128)(2,1)}, u32[]{:S(2)}) copy-start(bf16[256,1536]{1,0:T(8,128)(2,1)} %reduce-scatter.13.cloned.1.call-done) | copy-start | bytes 2359300
  852.6 73.5 %copy-start.40 = (f32[1536]{0:T(1024)S(1)}, f32[1536]{0:T(1024)}, u32[]{:S(2)}) copy-start(f32[1536]{0:T(1024)} %param.47) | copy-start | bytes 18436
  852.6 73.5 %copy-start.45 = (f32[256]{0:T(256)S(1)}, f32[256]{0:T(256)}, u32[]{:S(2)}) copy-start(f32[256]{0:T(256)} %copy-done.44) | copy-start | bytes 3076
  852.6 73.5 %copy-start.49 = (f32[256]{0:T(256)S(1)}, f32[256]{0:T(256)}, u32[]{:S(2)}) copy-start(f32[256]{0:T(256)} %copy-done.48) | copy-start | bytes 3076
  852.6 73.5 %copy-start.53 = (f32[256]{0:T(256)S(1)}, f32[256]{0:T(256)}, u32[]{:S(2)}) copy-start(f32[256]{0:T(256)} %copy-done.52) | copy-start | bytes 3076
  973.4 4.0 copy-start.1
  (27 other events, 64.6 us)
Sparse Core Ops, SparseCore 0:
  10.2 25.4 all-gather.17
  38.2 52.8 all-gather.13
  93.3 54.8 all-gather.15
  186.8 42.6 reduce-scatter.8
  231.8 43.8 all-gather.25
  277.8 38.2 all-gather.23
  318.2 63.5 all-gather.21
  384.3 42.4 all-gather.19
  454.6 43.8 reduce-scatter.12
  503.8 43.8 all-gather.27
  550.6 40.3 reduce-scatter.22
  593.2 69.0 reduce-scatter.20
  664.6 57.0 reduce-scatter.16
  723.4 29.3 all-gather.29
  754.9 32.9 reduce-scatter.18
  789.5 42.1 all-gather.33
  834.6 43.8 reduce-scatter.14
  881.4 44.6 reduce-scatter.10
  927.9 38.9 all-gather.31
